TPU v7x, 32 devices: a whole 2x2x4 slice. The times are simulated.
32 devices in a mesh: blk: 8 (over y, x, core), layer: 4 (over z).
Axes of the slice: x: 2, y: 2, z: 4, core: 2. Of those that a mesh axis runs over, the one named last changes fastest.
Arguments:
- points: float32 [8192, 128], P('blk'), may hold values from -6 to 6
- inv_scale: float32 [128], replicated, may hold values from 0.01 to 0.25
- vectors: float32 [8192, 64], P('blk'), may hold values from -6 to 6
- noise: float32 [8192], P(('blk', 'layer')), may hold values from 0.1 to 1
Outputs:
- result: float32 [8192, 64], P(('blk', 'layer'))
All inputs are finite; a program needn't handle non-finite values.
Results may differ from a plain program's by a relative error of at most 0.0001.
Values sent between devices are 32-bit elements; how exact they have to be, the bound alone decides.
A program may use at most 64 MiB of HBM per device.

v0:
```python
import jax
import jax.numpy as jnp
from jax import lax
from jax.sharding import PartitionSpec as P

ROOT_FIVE = 5.0**0.5
FIVE_THIRDS = 5.0 / 3.0


def passed_along(value, axis, steps):
    count = lax.axis_size(axis)
    pairs = [(source, (source + steps) % count) for source in range(count)]
    return lax.ppermute(value, axis, pairs)


def matern(left_scaled, right_scaled, right_norms):
    left_norms = jnp.sum(left_scaled * left_scaled, axis=1)
    cross = jnp.dot(
        left_scaled,
        right_scaled.T,
        precision=lax.Precision.HIGHEST,
        preferred_element_type=jnp.float32,
    )
    distance_sq = jnp.maximum(left_norms[:, None] + right_norms[None, :] - 2.0 * cross, 0.0)
    radius = jnp.sqrt(distance_sq)
    return (1.0 + ROOT_FIVE * radius + FIVE_THIRDS * distance_sq) * jnp.exp(-ROOT_FIVE * radius)


def per_device(points, inv_scale, vectors, noise):
    layers = lax.axis_size("layer")
    layer_index = lax.axis_index("layer")
    block_rows = points.shape[0]
    feature_count = points.shape[1]
    column_count = vectors.shape[1]
    piece_rows = block_rows // layers
    hop_count = layers.bit_length() - 1
    scaled = points * inv_scale[None, :]
    packed = jnp.concatenate([scaled, vectors], axis=1)
    partner = packed
    for bit_index in range(hop_count):
        shifted = passed_along(partner, "blk", -(1 << bit_index))
        partner = jnp.where(layer_index >> bit_index & 1 == 1, shifted, partner)
    partner_scaled = partner[:, :feature_count]
    partner_vectors = partner[:, feature_count:]
    partner_norms = jnp.sum(partner_scaled * partner_scaled, axis=1)
    tile_rows = min(512, block_rows)
    tile_count = block_rows // tile_rows
    query_scaled = scaled.reshape(tile_count, tile_rows, feature_count)
    query_vectors = vectors.reshape(tile_count, tile_rows, column_count)

    def visit(carry_sum, block_item):
        left_scaled, left_vectors = block_item
        kernel = matern(left_scaled, partner_scaled, partner_norms)
        direct = jnp.dot(
            kernel,
            partner_vectors,
            precision=lax.Precision.HIGHEST,
            preferred_element_type=jnp.float32,
        )
        carry_sum = carry_sum + lax.dot_general(
            kernel,
            left_vectors,
            (((0,), (0,)), ((), ())),
            precision=lax.Precision.HIGHEST,
            preferred_element_type=jnp.float32,
        )
        return (carry_sum, direct)

    mirrored, direct = lax.scan(
        visit, jnp.zeros((block_rows, column_count), jnp.float32), (query_scaled, query_vectors)
    )
    direct = direct.reshape(block_rows, column_count)
    mirrored = mirrored * (layer_index > 0).astype(jnp.float32)
    spread = lax.all_to_all(
        mirrored.reshape(layers, piece_rows, column_count),
        "layer",
        split_axis=0,
        concat_axis=0,
        tiled=True,
    )
    returned = jnp.zeros((piece_rows, column_count), jnp.float32)
    for distance in range(1, layers):
        returned = returned + passed_along(spread[distance], "blk", distance)
    own_sum = lax.psum_scatter(direct, "layer", scatter_dimension=0, tiled=True) + returned
    own_vectors = lax.dynamic_slice_in_dim(vectors, layer_index * piece_rows, piece_rows, 0)
    normalizer = float(block_rows * (2 * layers - 1)) ** (-0.5)
    return own_sum * normalizer + noise[:, None] * own_vectors


def solution(mesh):
    placed = (P("blk", None), P(), P("blk", None), P(("blk", "layer")))
    return jax.shard_map(
        per_device, mesh=mesh, in_specs=placed, out_specs=P(("blk", "layer"), None), check_vma=False
    )
```

profile of v0, /device:TPU:0, one launch (start us, length us, event | category | flops | bytes accessed | tf_op | source)
XLA Modules:
  0.0 104.9 jit_solution(11074152335680204316)
XLA Ops:
  6.5 1.3 %copy.13 = f32[1024,128]{0,1:T(8,128)S(1)} copy(f32[1024,128]{1,0:T(8,128)} %param.6) | data formatting | bytes 1048576 | tf_op args[0]
  8.7 3.4 %collective-permute-start = (f32[1024,192]{0,1:T(8,128)S(1)}, f32[1024,192]{0,1:T(8,128)S(1)}, u32[]{:S(2)}, u32[]{:S(2)}) collective-permute-start(f32[1024,192]{0,1:T(8,128)S(1)} %pad_maximum_fusion), channel_id=1, source_target_pairs={{0,28},{4,0},{8,4},{12,8},{16,12},{20,16},{24,20},{28,24},{1,29},{... | collective-permute-start | bytes 2359304 | tf_op jit(solution)/shard_map/ppermute | solution.py:13
  12.1 9.5 %collective-permute-done = f32[1024,192]{0,1:T(8,128)S(1)} collective-permute-done((f32[1024,192]{0,1:T(8,128)S(1)}, f32[1024,192]{0,1:T(8,128)S(1)}, u32[]{:S(2)}, u32[]{:S(2)}) %collective-permute-start) | collective-permute-done | bytes 786464 | tf_op jit(solution)/shard_map/ppermute | solution.py:13
  22.5 1.0 copy.14
  23.5 18.2 %collective-permute-done.1 = f32[1024,192]{0,1:T(8,128)S(1)} collective-permute-done((f32[1024,192]{0,1:T(8,128)S(1)}, f32[1024,192]{0,1:T(8,128)S(1)}, u32[]{:S(2)}, u32[]{:S(2)}) %collective-permute-start.1) | collective-permute-done | bytes 786464 | tf_op jit(solution)/shard_map/ppermute | solution.py:13
  43.1 24.9 %while.13 = (s32[]{:T(128)}, f32[1024,64]{0,1:T(8,128)S(1)}, f32[2,512,64]{1,0,2:T(2,128)}, f32[2,512,128]{2,1,0:T(8,128)S(1)}, f32[1024]{0:T(1024)S(1)}, /*inde...) while((s32[]{:T(128)}, f32[1024,64]{0,1:T(8,128)S(1)}, ...), condition=%wide.region_3.4_spmd.clone, body=%wide.region_1.3_spmd.clone.sunk | while | flops 1616117248 | bytes 9052795 | solution.py:69
  43.3 4.1 %exponential_multiply_fusion.2 = f32[512,1024]{1,0:T(8,128)S(1)} fusion(f32[1024,128]{1,0:T(8,128)} %get-tuple-element.180, f32[1024]{0:T(1024)S(1)} %get-tuple-element.179, f32[512]{0:T(512)S(1)} %fusion.25, f32[2,512,128]{2,1,0:T(8,128)S(1)} %get-tuple-element.178, s32[]{:T(128)} %get-tuple-element.165), kind=kOutput, calls=%fused_computation.clone.1 | convolution fusion | flops 810549248 | bytes 2889732 | tf_op jit(solution)/shard_map/while/body/eval_jaxpr/dot_general | solution.py:18
  47.3 2.5 %convolution_add_fusion.2 = f32[1024,64]{0,1:T(8,128)S(1)} fusion(f32[512,1024]{1,0:T(8,128)S(1)} %exponential_multiply_fusion.2, f32[1024,64]{0,1:T(8,128)S(1)} %get-tuple-element.166, f32[2,512,64]{2,1,0:T(8,128)} %get-tuple-element.181, s32[]{:T(128)} %get-tuple-element.165, pred[]{:T(512)S(6)} %compare.3), kind=kOutput, calls=%fused_computation.1.clone.1 | convolution fusion | flops 402784256 | bytes 2884097 | tf_op jit(solution)/shard_map/while/body/eval_jaxpr/dot_general | solution.py:60
  49.8 2.2 %convolution_bitcast_fusion.2 = f32[1,512,64]{1,2,0:T(8,128)S(1)} fusion(f32[512,1024]{1,0:T(8,128)S(1)} %exponential_multiply_fusion.2, f32[1024,64]{1,0:T(8,128)S(1)} %get-tuple-element.182), kind=kOutput, calls=%fused_computation.2.clone.1 | convolution fusion | flops 402653184 | bytes 2490368 | tf_op jit(solution)/shard_map/while/body/eval_jaxpr/dot_general | solution.py:54
  52.1 3.4 %dynamic_update_slice.6 = f32[2,512,64]{1,0,2:T(2,128)} dynamic-update-slice(f32[2,512,64]{1,0,2:T(2,128)} %get-tuple-element.167, f32[1,512,64]{1,0,2:T(1,128)S(1)} %copy.29, s32[]{:T(128)} %get-tuple-element.165, s32[]{:T(128)} %constant.6.clone.1..sunk, s32[]{:T(128)} %constant.6.clone.1..sunk) | dynamic-update-slice | bytes 262148 | tf_op jit(solution)/shard_map/while/body/jit(dynamic_update_index_in_dim)/dynamic_update_slice | solution.py:69
  55.7 4.1 %exponential_multiply_fusion.2 = f32[512,1024]{1,0:T(8,128)S(1)} fusion(f32[1024,128]{1,0:T(8,128)} %get-tuple-element.180, f32[1024]{0:T(1024)S(1)} %get-tuple-element.179, f32[512]{0:T(512)S(1)} %fusion.25, f32[2,512,128]{2,1,0:T(8,128)S(1)} %get-tuple-element.178, s32[]{:T(128)} %get-tuple-element.165), kind=kOutput, calls=%fused_computation.clone.1 | convolution fusion | flops 810549248 | bytes 2889732 | tf_op jit(solution)/shard_map/while/body/eval_jaxpr/dot_general | solution.py:18
  59.8 2.5 %convolution_add_fusion.2 = f32[1024,64]{0,1:T(8,128)S(1)} fusion(f32[512,1024]{1,0:T(8,128)S(1)} %exponential_multiply_fusion.2, f32[1024,64]{0,1:T(8,128)S(1)} %get-tuple-element.166, f32[2,512,64]{2,1,0:T(8,128)} %get-tuple-element.181, s32[]{:T(128)} %get-tuple-element.165, pred[]{:T(512)S(6)} %compare.3), kind=kOutput, calls=%fused_computation.1.clone.1 | convolution fusion | flops 402784256 | bytes 2884097 | tf_op jit(solution)/shard_map/while/body/eval_jaxpr/dot_general | solution.py:60
  62.2 2.2 %convolution_bitcast_fusion.2 = f32[1,512,64]{1,2,0:T(8,128)S(1)} fusion(f32[512,1024]{1,0:T(8,128)S(1)} %exponential_multiply_fusion.2, f32[1024,64]{1,0:T(8,128)S(1)} %get-tuple-element.182), kind=kOutput, calls=%fused_computation.2.clone.1 | convolution fusion | flops 402653184 | bytes 2490368 | tf_op jit(solution)/shard_map/while/body/eval_jaxpr/dot_general | solution.py:54
  64.5 3.4 %dynamic_update_slice.6 = f32[2,512,64]{1,0,2:T(2,128)} dynamic-update-slice(f32[2,512,64]{1,0,2:T(2,128)} %get-tuple-element.167, f32[1,512,64]{1,0,2:T(1,128)S(1)} %copy.29, s32[]{:T(128)} %get-tuple-element.165, s32[]{:T(128)} %constant.6.clone.1..sunk, s32[]{:T(128)} %constant.6.clone.1..sunk) | dynamic-update-slice | bytes 262148 | tf_op jit(solution)/shard_map/while/body/jit(dynamic_update_index_in_dim)/dynamic_update_slice | solution.py:69
  68.7 4.9 %all-to-all-start = ((f32[4,256,64]{1,2,0:T(8,128)}), f32[4,256,64]{1,2,0:T(8,128)S(1)}, u32[]{:S(2)}, u32[]{:S(2)}) async-start(f32[4,256,64]{1,2,0:T(8,128)} %bitcast.30), calls=%async_computation.1 | async-start | bytes 524288 | tf_op jit(solution)/shard_map/all_to_all | solution.py:74
  73.6 1.7 %copy.25 = f32[8,8,2,512]{3,1,2,0:T(8,128)} copy(f32[8,8,2,512]{3,2,1,0:T(2,128)} %bitcast.51) | data formatting | bytes 524288
  75.3 7.0 %all-to-all-done = f32[4,256,64]{1,2,0:T(8,128)S(1)} async-done(((f32[4,256,64]{1,2,0:T(8,128)}), f32[4,256,64]{1,2,0:T(8,128)S(1)}, u32[]{:S(2)}, u32[]{:S(2)}) %all-to-all-start) | async-done | bytes 262176 | tf_op jit(solution)/shard_map/all_to_all | solution.py:74
  82.4 1.2 %collective-permute-start.3 = (f32[256,64]{0,1:T(8,128)S(1)}, f32[256,64]{0,1:T(8,128)S(1)}, u32[]{:S(2)}, u32[]{:S(2)}) collective-permute-start(f32[256,64]{0,1:T(8,128)S(1)} %get-tuple-element.103), channel_id=1, source_target_pairs={{0,8},{4,12},{8,16},{12,20},{16,24},{20,28},{24,0},{28,4},{1,9},{5... | collective-permute-start | bytes 196616 | tf_op jit(solution)/shard_map/ppermute | solution.py:13
  83.6 1.8 %collective-permute-start.4 = (f32[256,64]{0,1:T(8,128)S(1)}, f32[256,64]{0,1:T(8,128)S(1)}, u32[]{:S(2)}, u32[]{:S(2)}) collective-permute-start(f32[256,64]{0,1:T(8,128)S(1)} %get-tuple-element.104), channel_id=1, source_target_pairs={{0,12},{4,16},{8,20},{12,24},{16,28},{20,0},{24,4},{28,8},{1,13},{... | collective-permute-start | bytes 196616 | tf_op jit(solution)/shard_map/ppermute | solution.py:13
  85.5 1.6 %collective-permute-done.2 = f32[256,64]{0,1:T(8,128)S(1)} collective-permute-done((f32[256,64]{0,1:T(8,128)S(1)}, f32[256,64]{0,1:T(8,128)S(1)}, u32[]{:S(2)}, u32[]{:S(2)}) %collective-permute-start.2) | collective-permute-done | bytes 65568 | tf_op jit(solution)/shard_map/ppermute | solution.py:13
  87.1 1.3 %collective-permute-done.3 = f32[256,64]{0,1:T(8,128)S(1)} collective-permute-done((f32[256,64]{0,1:T(8,128)S(1)}, f32[256,64]{0,1:T(8,128)S(1)}, u32[]{:S(2)}, u32[]{:S(2)}) %collective-permute-start.3) | collective-permute-done | bytes 65568 | tf_op jit(solution)/shard_map/ppermute | solution.py:13
  88.4 1.4 %collective-permute-done.4 = f32[256,64]{0,1:T(8,128)S(1)} collective-permute-done((f32[256,64]{0,1:T(8,128)S(1)}, f32[256,64]{0,1:T(8,128)S(1)}, u32[]{:S(2)}, u32[]{:S(2)}) %collective-permute-start.4) | collective-permute-done | bytes 65568 | tf_op jit(solution)/shard_map/ppermute | solution.py:13
  89.8 6.8 %reduce-scatter.2.cloned.1.call-done = f32[256,64]{0,1:T(8,128)} async-done(((f32[1024,64]{0,1:T(8,128)}), f32[256,64]{0,1:T(8,128)}) %reduce-scatter.2.cloned.1.call-update) | async-done | bytes 65552 | tf_op jit(solution)/shard_map/reduce_scatter | solution.py:84
  96.6 1.5 %multiply_add_fusion = f32[256,64]{0,1:T(8,128)} fusion(f32[1024,64]{0,1:T(8,128)} %param.8, s32[]{:T(128)S(6)} %select_n.21, f32[256,64]{0,1:T(8,128)} %reduce-scatter.2.cloned.1.call-done, f32[256,64]{0,1:T(8,128)S(1)} %collective-permute-done.4, f32[256,64]{0,1:T(8,128)S(1)} %collective-permute-done.2, f32[256,64]{0,1:T(8,128)S(1)} %collective-permute-done.3, ...), kind=kLoop, calls=%fused_computation.21 | loop fusion | flops 98304 | bytes 394244 | tf_op jit(solution)/shard_map/add | solution.py:87
  (26 shorter events, 4.5 us)
Async XLA Ops:
  6.5 2.1 %copy-start = (f32[1024,64]{0,1:T(8,128)S(1)}, f32[1024,64]{0,1:T(8,128)}, u32[]{:S(2)}) copy-start(f32[1024,64]{0,1:T(8,128)} %param.8) | copy-start | bytes 786436
  8.7 12.9 %collective-permute-start = (f32[1024,192]{0,1:T(8,128)S(1)}, f32[1024,192]{0,1:T(8,128)S(1)}, u32[]{:S(2)}, u32[]{:S(2)}) collective-permute-start(f32[1024,192]{0,1:T(8,128)S(1)} %pad_maximum_fusion), channel_id=1, source_target_pairs={{0,28},{4,0},{8,4},{12,8},{16,12},{20,16},{24,20},{28,24},{1,29},{... | collective-permute-start | bytes 2359304 | tf_op jit(solution)/shard_map/ppermute | solution.py:13
  21.7 20.0 %collective-permute-start.1 = (f32[1024,192]{0,1:T(8,128)S(1)}, f32[1024,192]{0,1:T(8,128)S(1)}, u32[]{:S(2)}, u32[]{:S(2)}) collective-permute-start(f32[1024,192]{0,1:T(8,128)S(1)} %broadcast_select_fusion), channel_id=1, source_target_pairs={{0,24},{4,28},{8,0},{12,4},{16,8},{20,12},{24,16},{28,20},{1,25},{... | collective-permute-start | bytes 2359304 | tf_op jit(solution)/shard_map/ppermute | solution.py:13
  68.0 28.6 %copy-start.1 = (f32[256]{0:T(256)S(1)}, f32[256]{0:T(256)}, u32[]{:S(2)}) copy-start(f32[256]{0:T(256)} %param.9) | copy-start | bytes 3076
  68.7 13.6 %all-to-all-start = ((f32[4,256,64]{1,2,0:T(8,128)}), f32[4,256,64]{1,2,0:T(8,128)S(1)}, u32[]{:S(2)}, u32[]{:S(2)}) async-start(f32[4,256,64]{1,2,0:T(8,128)} %bitcast.30), calls=%async_computation.1 | async-start | bytes 524288 | tf_op jit(solution)/shard_map/all_to_all | solution.py:74
  73.6 23.0 %reduce-scatter.2.cloned.1.call-start = ((), (), s32[]{:S(2)}) async-start(), calls=%async_computation.2 | async-start | bytes 327680 | tf_op jit(solution)/shard_map/reduce_scatter | solution.py:84
  82.4 4.7 %collective-permute-start.2 = (f32[256,64]{0,1:T(8,128)S(1)}, f32[256,64]{0,1:T(8,128)S(1)}, u32[]{:S(2)}, u32[]{:S(2)}) collective-permute-start(f32[256,64]{0,1:T(8,128)S(1)} %get-tuple-element.105), channel_id=1, source_target_pairs={{0,4},{4,8},{8,12},{12,16},{16,20},{20,24},{24,28},{28,0},{1,5},{5... | collective-permute-start | bytes 196616 | tf_op jit(solution)/shard_map/ppermute | solution.py:13
  82.4 6.0 %collective-permute-start.3 = (f32[256,64]{0,1:T(8,128)S(1)}, f32[256,64]{0,1:T(8,128)S(1)}, u32[]{:S(2)}, u32[]{:S(2)}) collective-permute-start(f32[256,64]{0,1:T(8,128)S(1)} %get-tuple-element.103), channel_id=1, source_target_pairs={{0,8},{4,12},{8,16},{12,20},{16,24},{20,28},{24,0},{28,4},{1,9},{5... | collective-permute-start | bytes 196616 | tf_op jit(solution)/shard_map/ppermute | solution.py:13
  83.6 6.2 %collective-permute-start.4 = (f32[256,64]{0,1:T(8,128)S(1)}, f32[256,64]{0,1:T(8,128)S(1)}, u32[]{:S(2)}, u32[]{:S(2)}) collective-permute-start(f32[256,64]{0,1:T(8,128)S(1)} %get-tuple-element.104), channel_id=1, source_target_pairs={{0,12},{4,16},{8,20},{12,24},{16,28},{20,0},{24,4},{28,8},{1,13},{... | collective-permute-start | bytes 196616 | tf_op jit(solution)/shard_map/ppermute | solution.py:13
Sparse Core Ops, SparseCore 0:
  76.7 19.8 reduce-scatter.1
where the time goes:
time: 106 us; the launch traced here: 105 us
  waiting for transfers between devices  45.8 us (43%)
  matrix products  17.3 us (16%)
  between operations  13.5 us (13%)
  local copies, waits for them, and re-layouts  13.3 us (13%)
  starting transfers between devices  12 us (11%)
  other arithmetic  2.93 us (3%)
    ppermute x5, waiting for transfers between devices, passed_along(): return lax.ppermute(value, axis, pairs)  32 us
    dot_general x2, matrix products, matern(): jnp.dot(left_scaled, right_scaled.T, precision=lax.Precision.HIGHEST, pre...  8.12 us
    dynamic_update_slice x4, local copies, waits for them, and re-layouts, per_device(): lax.scan(visit, jnp.zeros((block_rows, column_count), jnp.float32), (quer...  7.17 us
    ppermute x5, starting transfers between devices, passed_along(): return lax.ppermute(value, axis, pairs)  7.12 us
    all_to_all x1, waiting for transfers between devices, per_device(): lax.all_to_all(mirrored.reshape(layers, piece_rows, column_count), 'layer...  7 us
    reduce_scatter x1, waiting for transfers between devices, per_device(): lax.psum_scatter(direct, 'layer', scatter_dimension=0, tiled=True)  6.76 us
    unnamed x10, local copies, waits for them, and re-layouts  5.37 us
    dot_general x2, matrix products, visit(): lax.dot_general(kernel, left_vectors, (((0,), (0,)), ((), ())), precision...  4.91 us
  transfers between devices with their start and end apart: 7, of which 7 were waited for; matrix products, arithmetic and copies ran while one was open for 3% of the time, Pallas kernels for 0%

commit v1 on v0

v1 whole, which is shorter than its diff:
```python
import functools
import math

import jax
import jax.numpy as jnp
from jax import lax
from jax.experimental import pallas as pl
from jax.experimental.pallas import tpu as pltpu
from jax.sharding import PartitionSpec as P

MESH = pl.DeviceIdType.MESH
LOG2 = math.log(2.0)
UNIT = math.sqrt(5.0) / LOG2
BF16 = jnp.bfloat16
F32 = jnp.float32


def two_terms(value):
    high = value.astype(BF16).astype(F32)
    return high, (value - high).astype(BF16).astype(F32)


def augmented(points, scale, left):
    high, low = two_terms(points * scale)
    held = high + low
    norm = jnp.sum(held * held, axis=1, keepdims=True)
    first = norm.astype(BF16).astype(F32)
    second = (norm - first).astype(BF16).astype(F32)
    third = norm - first - second
    lane = lax.broadcasted_iota(jnp.int32, high.shape, 1)
    at, ones = (0, 3) if left else (3, 0)
    extra = jnp.where(
        lane == at,
        first,
        jnp.where(
            lane == at + 1,
            second,
            jnp.where(
                lane == at + 2,
                third,
                jnp.where((lane >= ones) & (lane < ones + 3), 1.0, 0.0),
            ),
        ),
    )
    if left:
        high, low = -2.0 * high, -2.0 * low
        terms = (high, high, low, extra)
    else:
        terms = (high, low, high, extra)
    return jnp.concatenate([term.astype(BF16) for term in terms], axis=1)


def nt_dot(left, right):
    return lax.dot_general(left, right, (((1,), (1,)), ((), ())), preferred_element_type=F32)


def kernel(
    blocks, layers, tile, points, scale, vectors, noise, out,
    p_own, v_own, p_in, v_in, left, v_left, direct, m_out, d_out, m_in, d_in,
    own_sem, p_send, v_send, p_recv, v_recv, pf_send, vf_send, m_send, m_recv, d_send, d_recv,
):
    block, layer = lax.axis_index("blk"), lax.axis_index("layer")
    core = lax.rem(block, 2)
    sibling = block + 1 - 2 * core
    rows, columns = p_own.shape[0], v_own.shape[0]
    piece = rows // layers

    def wrapped(index):
        return lax.rem(index + 2 * blocks, blocks)

    first_core = block - core
    partner = jnp.where(
        layer == 0,
        block,
        jnp.where(
            layer == 1,
            jnp.where(core == 0, block + 1, wrapped(block + layers - 1)),
            wrapped(first_core + layer),
        ),
    )
    shares = layer >= 2
    spreads = shares & (core == lax.rem(layer, 2))
    sends = (layer == 1) | spreads

    own_p = pltpu.make_async_copy(points, p_own, own_sem.at[0])
    own_v = pltpu.make_async_copy(vectors, v_own, own_sem.at[1])
    own_p.start()
    own_v.start()

    @pl.when(layer == 0)
    def _():
        for c in range(layers):
            at = pl.ds(c * piece, piece)
            pltpu.make_async_copy(points.at[at], p_in.at[c], p_recv.at[c]).start()
            pltpu.make_async_copy(vectors.at[:, at], v_in.at[c], v_recv.at[c]).start()

    barrier = pltpu.get_barrier_semaphore()

    def greet(to_block, to_layer):
        pl.semaphore_signal(barrier, inc=1, device_id=(to_block, to_layer), device_id_type=MESH)

    @pl.when(layer == 1)
    def _():
        greet(partner, layer)

    @pl.when(shares)
    def _():
        greet(partner, layer)
        greet(sibling, layer)

    for other in range(layers):

        @pl.when(layer != other)
        def _():
            greet(block, other)

    greet(wrapped(jnp.where(core == 1, block - 1, block - (layers - 1))), 1)
    for other in range(2, layers):

        @pl.when(core == other % 2)
        def _():
            greet(wrapped(block - other), other)
            greet(wrapped(block - other + 1), other)

    expected = layers - 1
    expected += jnp.where(layer >= 1, layers, 0) + jnp.where(sends, 1, 0)
    expected += jnp.where(shares, 1, 0) + jnp.where(spreads, 1, 0)
    pl.semaphore_wait(barrier, expected)

    own_p.wait()
    own_v.wait()

    def far(c):
        at = pl.ds(c * piece, piece)
        target = wrapped(
            jnp.where(
                layer == 1,
                jnp.where(core == 1, block - 1, block - (layers - 1)),
                block - layer + c % 2,
            )
        )
        return (
            pltpu.make_async_remote_copy(
                p_own.at[at], p_in.at[c], p_send.at[c], p_recv.at[c], (target, layer), MESH
            ),
            pltpu.make_async_remote_copy(
                v_own.at[:, at], v_in.at[c], v_send.at[c], v_recv.at[c], (target, layer), MESH
            ),
        )

    def near(c):
        return (
            pltpu.make_async_remote_copy(
                p_in.at[c], p_in.at[c], pf_send.at[c], p_recv.at[c], (sibling, layer), MESH
            ),
            pltpu.make_async_remote_copy(
                v_in.at[c], v_in.at[c], vf_send.at[c], v_recv.at[c], (sibling, layer), MESH
            ),
        )

    slot = jnp.where(layer == 1, 0, 1 + 2 * (layer // 2 - 1) + core)

    def mirrored_copy(c):
        return pltpu.make_async_remote_copy(
            m_out.at[c], m_in.at[slot], m_send.at[c], m_recv.at[slot], (partner, c), MESH
        )

    def direct_copy(c):
        return pltpu.make_async_remote_copy(
            d_out.at[c], d_in.at[layer], d_send.at[c], d_recv.at[layer], (block, c), MESH
        )

    @pl.when(sends)
    def _():
        for c in range(layers):
            for copy in far(c):
                copy.start()

    unit = scale[...] * UNIT
    left[...] = augmented(p_own[...], unit, True)
    v_left[...] = jnp.concatenate(two_terms(v_own[...]), axis=0).astype(BF16)

    for c in range(layers):
        pltpu.make_async_copy(p_in.at[c], p_in.at[c], p_recv.at[c]).wait()
        pltpu.make_async_copy(v_in.at[c], v_in.at[c], v_recv.at[c]).wait()

        @pl.when(shares & (core == c % 2))
        def _():
            for copy in near(c):
                copy.start()

        right = augmented(p_in[c], unit, False)
        v_right = jnp.concatenate(two_terms(v_in[c]), axis=0).T.astype(BF16)
        mirrored = None
        for start in range(0, rows, tile):
            at = pl.ds(start, tile)
            square = jnp.maximum(nt_dot(left[at, :], right), 1e-20)
            u = square * lax.rsqrt(square)
            value = (1.0 + u * (LOG2 + u * (LOG2 * LOG2 / 3.0))) * jnp.exp2(-u)
            high = value.astype(BF16)
            low = (value - high.astype(F32)).astype(BF16)
            term = jnp.dot(high, v_right, preferred_element_type=F32)
            term += jnp.dot(low, v_right, preferred_element_type=F32)
            if c == 0:
                direct[at, :] = term
            else:
                direct[at, :] += term
            turned = jnp.dot(v_left[:, at], high, preferred_element_type=F32)
            turned += jnp.dot(v_left[:, at], low, preferred_element_type=F32)
            mirrored = turned if mirrored is None else mirrored + turned
        m_out[c] = mirrored[:columns] + mirrored[columns:]

        @pl.when(layer >= 1)
        def _():
            mirrored_copy(c).start()

    for c in range(layers):
        turned = direct[pl.ds(c * piece, piece), :].T
        turned = turned[:columns] + turned[columns:]

        @pl.when(layer == c)
        def _():
            d_in[c] = turned

        @pl.when(layer != c)
        def _():
            d_out[c] = turned
            direct_copy(c).start()

    for s in range(layers - 1):
        pltpu.make_async_copy(m_in.at[s], m_in.at[s], m_recv.at[s]).wait()
    total = m_in[0]
    for s in range(1, layers - 1):
        total += m_in[s]
    for s in range(layers):

        @pl.when(layer != s)
        def _():
            pltpu.make_async_copy(d_in.at[s], d_in.at[s], d_recv.at[s]).wait()

    for s in range(layers):
        total += d_in[s]
    mine = v_own[:, pl.ds(pl.multiple_of(layer * piece, 128), piece)]
    normalizer = float(rows * (2 * layers - 1)) ** (-0.5)
    out[...] = total * normalizer + noise[...] * mine

    @pl.when(sends)
    def _():
        for c in range(layers):
            for copy in far(c):
                copy.wait_send()

    for c in range(layers):

        @pl.when(shares & (core == c % 2))
        def _():
            for copy in near(c):
                copy.wait_send()

        @pl.when(layer >= 1)
        def _():
            mirrored_copy(c).wait_send()

        @pl.when(layer != c)
        def _():
            direct_copy(c).wait_send()


def per_device(points, inv_scale, vectors, noise):
    blocks, layers = lax.axis_size("blk"), lax.axis_size("layer")
    rows, features = points.shape
    columns = vectors.shape[1]
    piece = rows // layers
    tile = min(256, rows)
    vmem = pl.BlockSpec(memory_space=pltpu.VMEM)
    hbm = pl.BlockSpec(memory_space=pl.ANY)
    dma = pltpu.SemaphoreType.DMA
    out = pl.pallas_call(
        functools.partial(kernel, blocks, layers, tile),
        out_shape=jax.ShapeDtypeStruct((columns, piece), F32),
        in_specs=[hbm, vmem, hbm, vmem],
        out_specs=vmem,
        scratch_shapes=[
            pltpu.VMEM((rows, features), F32),
            pltpu.VMEM((columns, rows), F32),
            pltpu.VMEM((layers, piece, features), F32),
            pltpu.VMEM((layers, columns, piece), F32),
            pltpu.VMEM((rows, 4 * features), BF16),
            pltpu.VMEM((2 * columns, rows), BF16),
            pltpu.VMEM((rows, 2 * columns), F32),
            pltpu.VMEM((layers, columns, piece), F32),
            pltpu.VMEM((layers, columns, piece), F32),
            pltpu.VMEM((layers - 1, columns, piece), F32),
            pltpu.VMEM((layers, columns, piece), F32),
            dma((2,)),
            *[dma((layers,)) for _ in range(7)],
            dma((layers - 1,)),
            dma((layers,)),
            dma((layers,)),
        ],
        compiler_params=pltpu.CompilerParams(collective_id=0, has_side_effects=True),
    )(points, inv_scale[None, :], vectors.T, noise[None, :])
    return out.T


def solution(mesh):
    placed = (P("blk", None), P(), P("blk", None), P(("blk", "layer")))
    return jax.shard_map(
        per_device, mesh=mesh, in_specs=placed, out_specs=P(("blk", "layer"), None), check_vma=False
    )
```

time: 106 us -> 29.2 us (0.28)
  waiting for transfers between devices: 45.8 us -> 0 us
  Pallas kernels: 0 us -> 27.6 us
  matrix products: 17.3 us -> 0 us
  between operations: 13.5 us -> 0.01 us
  starting transfers between devices: 12 us -> 0 us
  local copies, waits for them, and re-layouts: 13.3 us -> 1.47 us
  other arithmetic: 2.93 us -> 0 us
    ppermute x5 -> x0, waiting for transfers between devices: 32 us -> none  [passed_along(): return lax.ppermute(value, axis, pairs)]
    pallas_call x0 -> x1, Pallas kernels: none -> 27.6 us  [per_device(): pl.pallas_call(functools.partial(kernel, blocks, layers, tile), out_shape...]
    dot_general x6 -> x0, matrix products: 17.3 us -> none  [the longest x2 8.12 us: matern(): jnp.dot(left_scaled, right_scaled.T, precision=lax.Precision.HIGHEST, pre...]
    dynamic_update_slice x4 -> x0, local copies, waits for them, and re-layouts: 7.17 us -> none  [per_device(): lax.scan(visit, jnp.zeros((block_rows, column_count), jnp.float32), (quer...]
    ppermute x5 -> x0, starting transfers between devices: 7.12 us -> none  [passed_along(): return lax.ppermute(value, axis, pairs)]
    all_to_all x1 -> x0, waiting for transfers between devices: 7 us -> none  [per_device(): lax.all_to_all(mirrored.reshape(layers, piece_rows, column_count), 'layer...]
    reduce_scatter x1 -> x0, waiting for transfers between devices: 6.76 us -> none  [per_device(): lax.psum_scatter(direct, 'layer', scatter_dimension=0, tiled=True)]
    all_to_all x1 -> x0, starting transfers between devices: 4.87 us -> none  [per_device(): lax.all_to_all(mirrored.reshape(layers, piece_rows, column_count), 'layer...]
  transfers between devices with their start and end apart: 7 -> 0, of which waited for: 7 -> 0; matrix products, arithmetic and copies ran while one was open for 3% -> 0% of each run, Pallas kernels for 0% -> 0%
where the time goes in v1:
time: 29.2 us; the launch traced here: 29.1 us
  Pallas kernels  27.6 us (95%)
  local copies, waits for them, and re-layouts  1.47 us (5%)
    pallas_call x1, Pallas kernels, per_device(): pl.pallas_call(functools.partial(kernel, blocks, layers, tile), out_shape...  27.6 us
    unnamed x1, local copies, waits for them, and re-layouts  1.47 us

profile of v1, /device:TPU:0, one launch (start us, length us, event | category | flops | bytes accessed | tf_op | source)
XLA Modules:
  0.0 29.1 jit_solution(10952569165036293030)
XLA Ops:
  0.0 27.6 %shard_map.46 = f32[64,256]{1,0:T(8,128)} custom-call(f32[1024,128]{1,0:T(8,128)} %points.1, f32[1,128]{1,0:T(1,128)} %bitcast.7, f32[64,1024]{1,0:T(8,128)} %bitcast.5, f32[1,256]{1,0:T(1,128)} %bitcast.6), custom_call_target="tpu_custom_call" | custom-call | tf_op jit(solution)/shard_map/pallas_call | solution.py:278
  27.6 1.5 %copy.6 = f32[256,64]{0,1:T(8,128)} copy(f32[256,64]{0,1:T(8,128)} %bitcast.4) | data formatting | bytes 131072

commit v2 on v1

--- a/solution.py
+++ b/solution.py
@@ -56,8 +56,8 @@
 
 def kernel(
     blocks, layers, tile, points, scale, vectors, noise, out,
-    p_own, v_own, p_in, v_in, left, v_left, direct, m_out, d_out, m_in, d_in,
-    own_sem, p_send, v_send, p_recv, v_recv, pf_send, vf_send, m_send, m_recv, d_send, d_recv,
+    p_own, v_own, p_in, v_in, left, v_left, direct, m_out, d_out, m_in, d_in, m_near, m_sum,
+    own_sem, p_send, v_send, p_recv, v_recv, pf_send, vf_send, m_send, m_recv, d_send, d_recv, mn_send, mn_recv,
 ):
     block, layer = lax.axis_index("blk"), lax.axis_index("layer")
     core = lax.rem(block, 2)
@@ -119,11 +119,10 @@
 
         @pl.when(core == other % 2)
         def _():
-            greet(wrapped(block - other), other)
-            greet(wrapped(block - other + 1), other)
+            greet(wrapped(block - other + lax.rem(layer, 2)), other)
 
     expected = layers - 1
-    expected += jnp.where(layer >= 1, layers, 0) + jnp.where(sends, 1, 0)
+    expected += jnp.where(shares, layers // 2, jnp.where(layer == 1, layers, 0)) + jnp.where(sends, 1, 0)
     expected += jnp.where(shares, 1, 0) + jnp.where(spreads, 1, 0)
     pl.semaphore_wait(barrier, expected)
 
@@ -158,12 +157,24 @@
             ),
         )
 
-    slot = jnp.where(layer == 1, 0, 1 + 2 * (layer // 2 - 1) + core)
+    slot = layer // 2
 
     def mirrored_copy(c):
         return pltpu.make_async_remote_copy(
-            m_out.at[c], m_in.at[slot], m_send.at[c], m_recv.at[slot], (partner, c), MESH
-        )
+            m_sum.at[c], m_in.at[slot], m_send.at[c], m_recv.at[slot], (partner, c), MESH
+        )
+
+    def mirrored_near(c):
+        return pltpu.make_async_remote_copy(
+            m_out.at[c], m_near.at[c], mn_send.at[c], mn_recv.at[c], (sibling, layer), MESH
+        )
+
+    def join(c):
+        @pl.when(shares & (core == c % 2))
+        def _():
+            pltpu.make_async_copy(m_near.at[c], m_near.at[c], mn_recv.at[c]).wait()
+            m_sum[c] = m_sum[c] + m_near[c]
+            mirrored_copy(c).start()
 
     def direct_copy(c):
         return pltpu.make_async_remote_copy(
@@ -208,11 +219,23 @@
             turned = jnp.dot(v_left[:, at], high, preferred_element_type=F32)
             turned += jnp.dot(v_left[:, at], low, preferred_element_type=F32)
             mirrored = turned if mirrored is None else mirrored + turned
-        m_out[c] = mirrored[:columns] + mirrored[columns:]
-
-        @pl.when(layer >= 1)
+        mirrored = mirrored[:columns] + mirrored[columns:]
+
+        @pl.when(shares & (core != c % 2))
+        def _():
+            m_out[c] = mirrored
+            mirrored_near(c).start()
+
+        @pl.when(jnp.logical_not(shares & (core != c % 2)))
+        def _():
+            m_sum[c] = mirrored
+
+        @pl.when(layer == 1)
         def _():
             mirrored_copy(c).start()
+
+        if c > 0:
+            join(c - 1)
 
     for c in range(layers):
         turned = direct[pl.ds(c * piece, piece), :].T
@@ -227,10 +250,11 @@
             d_out[c] = turned
             direct_copy(c).start()
 
-    for s in range(layers - 1):
+    join(layers - 1)
+    for s in range(layers // 2):
         pltpu.make_async_copy(m_in.at[s], m_in.at[s], m_recv.at[s]).wait()
     total = m_in[0]
-    for s in range(1, layers - 1):
+    for s in range(1, layers // 2):
         total += m_in[s]
     for s in range(layers):
 
@@ -257,9 +281,13 @@
             for copy in near(c):
                 copy.wait_send()
 
-        @pl.when(layer >= 1)
+        @pl.when((layer == 1) | (shares & (core == c % 2)))
         def _():
             mirrored_copy(c).wait_send()
+
+        @pl.when(shares & (core != c % 2))
+        def _():
+            mirrored_near(c).wait_send()
 
         @pl.when(layer != c)
         def _():
@@ -290,13 +318,14 @@
             pltpu.VMEM((rows, 2 * columns), F32),
             pltpu.VMEM((layers, columns, piece), F32),
             pltpu.VMEM((layers, columns, piece), F32),
-            pltpu.VMEM((layers - 1, columns, piece), F32),
+            pltpu.VMEM((layers // 2, columns, piece), F32),
+            pltpu.VMEM((layers, columns, piece), F32),
+            pltpu.VMEM((layers, columns, piece), F32),
             pltpu.VMEM((layers, columns, piece), F32),
             dma((2,)),
             *[dma((layers,)) for _ in range(7)],
-            dma((layers - 1,)),
-            dma((layers,)),
-            dma((layers,)),
+            dma((layers // 2,)),
+            *[dma((layers,)) for _ in range(4)],
         ],
         compiler_params=pltpu.CompilerParams(collective_id=0, has_side_effects=True),
     )(points, inv_scale[None, :], vectors.T, noise[None, :])

time: 29.2 us -> 29.3 us (level)
  no operation moved by 1% of the time
where the time goes in v2:
time: 29.3 us; the launch traced here: 29.2 us
  Pallas kernels  27.7 us (95%)
  local copies, waits for them, and re-layouts  1.47 us (5%)
    pallas_call x1, Pallas kernels, per_device(): pl.pallas_call(functools.partial(kernel, blocks, layers, tile), out_shape...  27.7 us
    unnamed x1, local copies, waits for them, and re-layouts  1.47 us

profile of v2, /device:TPU:0, one launch (start us, length us, event | category | flops | bytes accessed | tf_op | source)
XLA Modules:
  0.0 29.2 jit_solution(7257350297023958604)
XLA Ops:
  0.0 27.7 %shard_map.46 = f32[64,256]{1,0:T(8,128)} custom-call(f32[1024,128]{1,0:T(8,128)} %points.1, f32[1,128]{1,0:T(1,128)} %bitcast.7, f32[64,1024]{1,0:T(8,128)} %bitcast.5, f32[1,256]{1,0:T(1,128)} %bitcast.6), custom_call_target="tpu_custom_call" | custom-call | tf_op jit(solution)/shard_map/pallas_call | solution.py:306
  27.7 1.5 %copy.6 = f32[256,64]{0,1:T(8,128)} copy(f32[256,64]{0,1:T(8,128)} %bitcast.4) | data formatting | bytes 131072
